TPU v7x, 256 devices: a whole 4x4x8 slice. The times are simulated.
256 devices in a mesh: grp: 8 (over z_hi, x), sub: 32 (over z_lo, y, core).
Axes of the slice: x: 4, y: 4, z: 8 (z_hi: 2, z_lo: 4; z = z_hi * 4 + z_lo), core: 2. Of those that a mesh axis runs over, the one named last changes fastest.
Arguments:
- counts: int32 [256], P(('grp', 'sub')), may hold values from 1 to 3, as said below
- block_map: int32 [768], P(('grp', 'sub')), may hold values from 0 to 31
- perms: int32 [768, 256], P(('grp', 'sub')), may hold values from 0 to 255, each once within a row
- mass_ii: bfloat16 [768, 1024, 1024], P(('grp', 'sub')), may hold values from -0.005859375 to 0.005859375
- mass_ib: bfloat16 [768, 1024, 256], P(('grp', 'sub')), may hold values from -0.1875 to 0.1875
- mass_bb: bfloat16 [768, 256, 256], P(('grp', 'sub')), may hold values from -6 to 6
- constraint_modes: bfloat16 [768, 1024, 256], P(('grp', 'sub')), may hold values from -6 to 6
- fixed_modes: bfloat16 [768, 1024, 128], P(('grp', 'sub')), may hold values from -6 to 6
Outputs:
- blocks: float32 [128, 256, 256], P('grp', 'sub')
- coupling: float32 [768, 128, 256], P(('grp', 'sub'))
Inputs may be any that keep to these rules, and one draw needn't show every extreme that they name: `counts`: at least one device uses all 3 slots and one uses a single slot.
All inputs are finite; a program needn't handle non-finite values.
Results may differ from a plain program's by a relative error of at most 0.0021.
Values sent between devices are 32-bit elements; how exact they have to be, the bound alone decides.
A program may use at most 128 MiB of HBM per device.

v0:
```python
import jax
import jax.numpy as jnp
from jax import lax
from jax.sharding import PartitionSpec as P

NBG = 16


def shifted(value, axis, by):
    peers = lax.axis_size(axis)
    return lax.ppermute(value, axis, [(i, (i + by) % peers) for i in range(peers)])


def contract(left, right):
    return lax.dot_general(
        left, right, (((0,), (0,)), ((), ())), preferred_element_type=jnp.float32
    )


def reduce_slot(mass_ii, mass_ib, mass_bb, constraint_modes, fixed_modes):
    product = jnp.dot(mass_ii, constraint_modes, preferred_element_type=jnp.float32).astype(
        jnp.bfloat16
    )
    cross = contract(constraint_modes, mass_ib)
    reduced = contract(constraint_modes, product) + cross + cross.T + mass_bb.astype(jnp.float32)
    coupled = contract(fixed_modes, product) + contract(fixed_modes, mass_ib)
    return (reduced, coupled)


def per_device(counts, block_map, perms, mass_ii, mass_ib, mass_bb, constraint_modes, fixed_modes):
    width = mass_bb.shape[1]
    modes = fixed_modes.shape[2]
    slot_total = mass_ii.shape[0]
    used_count = counts[0]
    sub_size = lax.axis_size("sub")

    def pick(array, slot_index):
        return lax.dynamic_index_in_dim(array, slot_index, 0, keepdims=False)

    start_parts = jnp.zeros((slot_total, width, width), jnp.float32)
    carry_state = (start_parts, jnp.zeros((slot_total, modes, width), jnp.float32))
    for slot_index in range(slot_total):
        one_parts, one_coupling = carry_state
        reduced, coupled = reduce_slot(
            pick(mass_ii, slot_index),
            pick(mass_ib, slot_index),
            pick(mass_bb, slot_index),
            pick(constraint_modes, slot_index),
            pick(fixed_modes, slot_index),
        )
        active = (slot_index < used_count).astype(jnp.float32)
        perm_row = pick(perms, slot_index)
        inverse = (
            jnp.zeros((width,), jnp.int32).at[perm_row].set(jnp.arange(width, dtype=jnp.int32))
        )
        placed = reduced[inverse][:, inverse] * active
        one_parts = lax.dynamic_update_index_in_dim(one_parts, placed, slot_index, 0)
        one_coupling = lax.dynamic_update_index_in_dim(
            one_coupling, coupled * active, slot_index, 0
        )
        carry_state = (one_parts, one_coupling)
    parts, coupling = carry_state
    slot_ids = jnp.arange(slot_total, dtype=jnp.int32)
    active_col = (slot_ids < used_count).astype(jnp.float32)
    targets = jnp.arange(2 * NBG, dtype=jnp.int32)
    one_hot = (block_map[:, None] == targets[None, :]).astype(jnp.float32) * active_col[:, None]
    spread_hot = jnp.broadcast_to(one_hot[:, None, :], (slot_total, sub_size, 2 * NBG))
    rows_in, hot_in = (
        lax.all_to_all(parts, "sub", split_axis=1, concat_axis=0, tiled=True),
        lax.all_to_all(spread_hot, "sub", split_axis=1, concat_axis=0, tiled=True),
    )
    hot_flat = hot_in[:, 0, :]
    owned = jnp.einsum("rc,rab->cab", hot_flat, rows_in, precision=lax.Precision.HIGHEST)
    home_rows = owned[:NBG]
    ahead_rows = owned[NBG:]
    blocks = home_rows + shifted(ahead_rows, "grp", 1)
    return (blocks, coupling)


def solution(mesh):
    placed = (
        P(("grp", "sub")),
        P(("grp", "sub")),
        P(("grp", "sub"), None),
        P(("grp", "sub"), None, None),
        P(("grp", "sub"), None, None),
        P(("grp", "sub"), None, None),
        P(("grp", "sub"), None, None),
        P(("grp", "sub"), None, None),
    )
    return jax.shard_map(
        per_device,
        mesh=mesh,
        in_specs=placed,
        out_specs=(P("grp", "sub", None), P(("grp", "sub"), None, None)),
        check_vma=False,
    )
```

profile of v0, /device:TPU:8, one launch (start us, length us, event | category | flops | bytes accessed | tf_op | source)
XLA Modules:
  0.0 108.0 jit_solution(16214703957208074257)
XLA Ops:
  2.8 9.2 %all-to-all-start = ((f32[3,32,32]{2,0,1:T(4,128)}), f32[3,32,32]{2,0,1:T(4,128)}, u32[]{:S(2)}, u32[]{:S(2)}) async-start(f32[3,32,32]{2,0,1:T(4,128)} %broadcast_in_dim.40), calls=%async_computation | async-start | bytes 131072 | tf_op jit(solution)/shard_map/all_to_all | solution.py:70
  12.0 2.2 %fusion.50 = f32[256,256]{1,0:T(8,128)} fusion(bf16[3,1024,256]{2,1,0:T(8,128)(2,1)} %param.12, bf16[3,1024,256]{2,1,0:T(8,128)(2,1)} %param.14), kind=kOutput, calls=%fused_computation.63 | convolution fusion | flops 134217728 | bytes 1310720 | tf_op jit(solution)/shard_map/dot_general | solution.py:15
  14.2 2.1 %fusion.38 = f32[256,256]{1,0:T(8,128)} fusion(bf16[3,1024,256]{2,1,0:T(8,128)(2,1)} %param.12, bf16[3,1024,256]{2,1,0:T(8,128)(2,1)S(1)} %copy-done), kind=kOutput, calls=%fused_computation.51 | convolution fusion | flops 134217728 | bytes 1310720 | tf_op jit(solution)/shard_map/dot_general | solution.py:15
  16.3 1.5 %fusion.44 = f32[256,256]{1,0:T(8,128)S(1)} fusion(bf16[3,1024,256]{2,1,0:T(8,128)(2,1)} %param.12, bf16[3,1024,256]{2,1,0:T(8,128)(2,1)S(1)} %copy-done), kind=kOutput, calls=%fused_computation.57 | convolution fusion | flops 134217728 | bytes 1310720 | tf_op jit(solution)/shard_map/dot_general | solution.py:15
  17.8 2.8 %fusion.9 = bf16[1024,256]{1,0:T(8,128)(2,1)S(1)} fusion(bf16[3,1024,1024]{2,1,0:T(8,128)(2,1)} %param.11, bf16[3,1024,256]{2,1,0:T(8,128)(2,1)S(1)} %copy-done), kind=kOutput, calls=%fused_computation.18 | convolution fusion | flops 537133056 | bytes 3145728 | tf_op jit(solution)/shard_map/dot_general | solution.py:21
  22.1 1.4 %scatter_custom_fusion = s32[256]{0:T(256)S(1)} fusion(s32[256]{0:T(256)S(1)} %bitcast.174, s32[256]{0:T(256)S(1)} %iota.22, s32[]{:T(128)} %constant.74.clone.1), kind=kCustom, calls=%fused_computation.116 | custom fusion | bytes 1028 | tf_op jit(solution)/shard_map/scatter | solution.py:54
  23.6 1.4 %scatter_custom_fusion.1 = s32[256]{0:T(256)S(1)} fusion(s32[256]{0:T(256)S(1)} %bitcast.173, s32[256]{0:T(256)S(1)} %iota.23, s32[]{:T(128)} %constant.74.clone.1), kind=kCustom, calls=%fused_computation.114 | custom fusion | bytes 1028 | tf_op jit(solution)/shard_map/scatter | solution.py:54
  25.0 1.4 %scatter_custom_fusion.2 = s32[256]{0:T(256)S(1)} fusion(s32[256]{0:T(256)S(1)} %bitcast.172, s32[256]{0:T(256)S(1)} %iota.24, s32[]{:T(128)} %constant.74.clone.1), kind=kCustom, calls=%fused_computation.112 | custom fusion | bytes 1028 | tf_op jit(solution)/shard_map/scatter | solution.py:54
  27.3 1.8 %copy.57 = f32[256,256]{0,1:T(8,128)} copy(f32[256,256]{1,0:T(8,128)} %fusion.38) | data formatting | bytes 524288 | tf_op jit(solution)/shard_map/dot_general | solution.py:15
  29.1 1.8 %copy.49 = f32[256,256]{0,1:T(8,128)} copy(f32[256,256]{1,0:T(8,128)} %fusion.50) | data formatting | bytes 524288 | tf_op jit(solution)/shard_map/dot_general | solution.py:15
  30.9 1.7 %fusion.90 = (bf16[1,256,256]{2,1,0:T(8,128)(2,1)}, bf16[1,256,256]{2,1,0:T(8,128)(2,1)}, bf16[1,256,256]{2,1,0:T(8,128)(2,1)S(1)}) fusion(bf16[3,256,256]{2,1,0:T(8,128)(2,1)} %param.13), kind=kLoop, calls=%fused_computation.118 | loop fusion | bytes 786432 | tf_op jit(solution)/shard_map/jit(dynamic_index_in_dim)/dynamic_slice | solution.py:38
  32.7 1.7 %copy.78 = bf16[1,256,256]{1,2,0:T(8,128)(2,1)} copy(bf16[1,256,256]{2,1,0:T(8,128)(2,1)} %get-tuple-element.8) | data formatting | bytes 262144
  34.3 1.7 %copy.77 = bf16[1,256,256]{1,2,0:T(8,128)(2,1)} copy(bf16[1,256,256]{2,1,0:T(8,128)(2,1)} %get-tuple-element.9) | data formatting | bytes 262144
  36.7 2.0 %fusion.26 = f32[256,256]{0,1:T(8,128)} fusion(f32[256,256]{0,1:T(8,128)} %copy.49, bf16[1024,256]{1,0:T(8,128)(2,1)S(1)} %fusion.9, bf16[3,1024,256]{2,1,0:T(8,128)(2,1)S(1)} %copy-done, f32[256,256]{1,0:T(8,128)S(1)} %copy-done.4, bf16[1,256,256]{1,2,0:T(8,128)(2,1)} %copy.76), kind=kOutput, calls=%fused_computation.32 | convolution fusion | flops 134479872 | bytes 1966080 | tf_op jit(solution)/shard_map/dot_general | solution.py:15
  38.8 1.1 copy.51
  39.9 1.7 %gather_fusion = f32[256,256]{1,0:T(8,128)} fusion(f32[256,256]{1,0:T(8,128)S(1)} %copy.51, s32[1024]{0:T(1024)S(1)} %pad_clamp_fusion.2), kind=kCustom, calls=%fused_computation | custom fusion | bytes 525312 | tf_op jit(solution)/shard_map/gather | solution.py:56
  41.5 1.1 %copy.52 = f32[256,256]{0,1:T(8,128)S(1)} copy(f32[256,256]{1,0:T(8,128)} %gather_fusion) | data formatting | bytes 524288 | tf_op jit(solution)/shard_map/gather | solution.py:56
  42.6 1.7 %gather_fusion.1 = f32[256,256]{1,0:T(8,128)} fusion(f32[256,256]{0,1:T(8,128)S(1)} %copy.52, s32[1024]{0:T(1024)S(1)} %pad_clamp_fusion.2), kind=kCustom, calls=%fused_computation.1 | custom fusion | bytes 525312 | tf_op jit(solution)/shard_map/gather | solution.py:56
  44.3 2.1 %fusion.22 = f32[256,256]{0,1:T(8,128)} fusion(f32[256,256]{0,1:T(8,128)} %copy.57, bf16[1024,256]{1,0:T(8,128)(2,1)S(1)} %fusion.15, bf16[3,1024,256]{2,1,0:T(8,128)(2,1)S(1)} %copy-done, f32[256,256]{1,0:T(8,128)} %fusion.38, bf16[1,256,256]{1,2,0:T(8,128)(2,1)S(1)} %copy-done.7), kind=kOutput, calls=%fused_computation.28 | convolution fusion | flops 134479872 | bytes 1966080 | tf_op jit(solution)/shard_map/dot_general | solution.py:15
  47.5 1.7 %gather_fusion.4 = f32[256,256]{1,0:T(8,128)} fusion(f32[256,256]{1,0:T(8,128)S(1)} %copy.59, s32[1024]{0:T(1024)S(1)} %pad_clamp_fusion), kind=kCustom, calls=%fused_computation.4 | custom fusion | bytes 525312 | tf_op jit(solution)/shard_map/gather | solution.py:56
  49.1 1.1 %copy.60 = f32[256,256]{0,1:T(8,128)S(1)} copy(f32[256,256]{1,0:T(8,128)} %gather_fusion.4) | data formatting | bytes 524288 | tf_op jit(solution)/shard_map/gather | solution.py:56
  50.3 1.7 %gather_fusion.5 = f32[256,256]{1,0:T(8,128)} fusion(f32[256,256]{0,1:T(8,128)S(1)} %copy.60, s32[1024]{0:T(1024)S(1)} %pad_clamp_fusion), kind=kCustom, calls=%fused_computation.5 | custom fusion | bytes 525312 | tf_op jit(solution)/shard_map/gather | solution.py:56
  51.9 1.4 %fusion.24 = f32[256,256]{0,1:T(8,128)S(1)} fusion(f32[256,256]{0,1:T(8,128)} %copy.53, bf16[1024,256]{1,0:T(8,128)(2,1)S(1)} %fusion.12, bf16[3,1024,256]{2,1,0:T(8,128)(2,1)S(1)} %copy-done, f32[256,256]{1,0:T(8,128)} %copy-done.3, bf16[1,256,256]{1,2,0:T(8,128)(2,1)S(1)} %copy-done.6), kind=kOutput, calls=%fused_computation.30 | convolution fusion | flops 134479872 | bytes 1966080 | tf_op jit(solution)/shard_map/dot_general | solution.py:15
  56.5 1.3 %copy.61 = f32[3,256,256]{2,0,1:T(4,128)} copy(f32[3,256,256]{1,2,0:T(8,128)S(1)} %bitcast_dynamic-update-slice_fusion) | data formatting | bytes 1572864 | tf_op jit(solution)/shard_map/jit(dynamic_update_index_in_dim)/dynamic_update_slice | solution.py:57
  57.8 7.7 %all-to-all-start.1 = ((f32[3,256,256]{2,0,1:T(4,128)}), f32[3,256,256]{2,0,1:T(4,128)S(1)}, u32[]{:S(2)}, u32[]{:S(2)}) async-start(f32[3,256,256]{2,0,1:T(4,128)} %copy.61), calls=%async_computation.1 | async-start | bytes 2097152 | tf_op jit(solution)/shard_map/all_to_all | solution.py:69
  65.6 1.4 %convolution_bitcast_fusion.5 = f32[128,256]{0,1:T(8,128)S(1)} fusion(bf16[1024,256]{1,0:T(8,128)(2,1)S(1)} %fusion.9, bf16[3,1024,128]{2,1,0:T(8,128)(2,1)} %param.15), kind=kOutput, calls=%fused_computation.46 | convolution fusion | flops 67108864 | bytes 917504 | tf_op jit(solution)/shard_map/dot_general | solution.py:15
  66.9 1.5 %fusion.34 = f32[1,128,256]{1,2,0:T(8,128)S(1)} fusion(f32[128,256]{0,1:T(8,128)S(1)} %convolution_bitcast_fusion.5, bf16[3,1024,256]{2,1,0:T(8,128)(2,1)} %param.12, bf16[3,1024,128]{2,1,0:T(8,128)(2,1)} %param.15, f32[]{:T(128)S(6)} %convert_element_type.48), kind=kOutput, calls=%fused_computation.45 | convolution fusion | flops 67174400 | bytes 1048580 | tf_op jit(solution)/shard_map/dot_general | solution.py:15
  69.1 1.4 %fusion.32 = f32[3,128,256]{1,2,0:T(8,128)S(1)} fusion(f32[3,128,256]{1,2,0:T(8,128)S(1)} %dynamic_update_slice.23, f32[128,256]{0,1:T(8,128)S(1)} %convolution_bitcast_fusion.4, bf16[3,1024,256]{2,1,0:T(8,128)(2,1)} %param.12, bf16[3,1024,128]{2,1,0:T(8,128)(2,1)S(1)} %copy-done.5, f32[]{:T(128)S(6)} %convert_element_type.52), kind=kOutput, calls=%fused_computation.41 | convolution fusion | flops 67174400 | bytes 1048580 | tf_op jit(solution)/shard_map/dot_general | solution.py:15
  71.4 20.0 %all-to-all-done.1 = f32[3,256,256]{2,0,1:T(4,128)S(1)} async-done(((f32[3,256,256]{2,0,1:T(4,128)}), f32[3,256,256]{2,0,1:T(4,128)S(1)}, u32[]{:S(2)}, u32[]{:S(2)}) %all-to-all-start.1) | async-done | bytes 786464 | tf_op jit(solution)/shard_map/all_to_all | solution.py:69
  92.4 1.6 %collective-permute-start = (f32[16,8,256]{2,0,1:T(8,128)S(1)}, f32[16,8,256]{2,0,1:T(8,128)S(1)}, u32[]{:S(2)}, u32[]{:S(2)}) collective-permute-start(f32[16,8,256]{2,0,1:T(8,128)S(1)} %slice.39), channel_id=1, source_target_pairs={{0,32},{32,64},{64,96},{96,128},{128,160},{160,192},{192,224},{224... | collective-permute-start | bytes 393224 | tf_op jit(solution)/shard_map/ppermute | solution.py:11
  94.0 1.5 %fusion.29 = f32[3,128,256]{1,2,0:T(8,128)S(1)} fusion(f32[3,128,256]{1,2,0:T(8,128)S(1)} %fusion.32, f32[128,256]{0,1:T(8,128)S(1)} %convolution_bitcast_fusion.3, bf16[3,1024,256]{2,1,0:T(8,128)(2,1)} %param.12, bf16[3,1024,128]{2,1,0:T(8,128)(2,1)} %param.15, f32[]{:T(128)S(6)} %convert_element_type.56), kind=kOutput, calls=%fused_computation.36 | convolution fusion | flops 67174400 | bytes 1048580 | tf_op jit(solution)/shard_map/dot_general | solution.py:15
  96.4 10.9 %collective-permute-done = f32[16,8,256]{2,0,1:T(8,128)S(1)} collective-permute-done((f32[16,8,256]{2,0,1:T(8,128)S(1)}, f32[16,8,256]{2,0,1:T(8,128)S(1)}, u32[]{:S(2)}, u32[]{:S(2)}) %collective-permute-start) | collective-permute-done | bytes 131104 | tf_op jit(solution)/shard_map/ppermute | solution.py:11
  (57 shorter events, 12.9 us)
Async XLA Ops:
  0.6 13.6 %copy-start = (bf16[3,1024,256]{2,1,0:T(8,128)(2,1)S(1)}, bf16[3,1024,256]{2,1,0:T(8,128)(2,1)}, u32[]{:S(2)}) copy-start(bf16[3,1024,256]{2,1,0:T(8,128)(2,1)} %param.14) | copy-start | bytes 4718596
  2.8 55.0 %all-to-all-start = ((f32[3,32,32]{2,0,1:T(4,128)}), f32[3,32,32]{2,0,1:T(4,128)}, u32[]{:S(2)}, u32[]{:S(2)}) async-start(f32[3,32,32]{2,0,1:T(4,128)} %broadcast_in_dim.40), calls=%async_computation | async-start | bytes 131072 | tf_op jit(solution)/shard_map/all_to_all | solution.py:70
  16.3 4.3 %copy-start.9 = (bf16[3,1024,1024]{2,1,0:T(8,128)(2,1)S(1)}, bf16[3,1024,1024]{2,1,0:T(8,128)(2,1)}, u32[]{:S(2)}) copy-start(bf16[3,1024,1024]{2,1,0:T(8,128)(2,1)} %param.11) | copy-start | bytes 18874372
  17.8 8.6 %copy-start.3 = (f32[256,256]{1,0:T(8,128)}, f32[256,256]{1,0:T(8,128)S(1)}, u32[]{:S(2)}) copy-start(f32[256,256]{1,0:T(8,128)S(1)} %fusion.44) | copy-start | bytes 786436
  21.3 0.7 copy-start.8
  27.3 9.5 %copy-start.4 = (f32[256,256]{1,0:T(8,128)S(1)}, f32[256,256]{1,0:T(8,128)}, u32[]{:S(2)}) copy-start(f32[256,256]{1,0:T(8,128)} %fusion.50) | copy-start | bytes 786436
  41.5 2.8 %copy-start.7 = (bf16[1,256,256]{1,2,0:T(8,128)(2,1)S(1)}, bf16[1,256,256]{1,2,0:T(8,128)(2,1)}, u32[]{:S(2)}) copy-start(bf16[1,256,256]{1,2,0:T(8,128)(2,1)} %copy.78) | copy-start | bytes 393220
  49.1 2.8 %copy-start.6 = (bf16[1,256,256]{1,2,0:T(8,128)(2,1)S(1)}, bf16[1,256,256]{1,2,0:T(8,128)(2,1)}, u32[]{:S(2)}) copy-start(bf16[1,256,256]{1,2,0:T(8,128)(2,1)} %copy.77) | copy-start | bytes 393220
  54.4 1.1 %copy-start.1 = (f32[256,256]{1,0:T(8,128)S(1)}, f32[256,256]{1,0:T(8,128)}, u32[]{:S(2)}) copy-start(f32[256,256]{1,0:T(8,128)} %gather_fusion.1) | copy-start | bytes 786436
  55.5 1.0 copy-start.2
  57.8 33.6 %all-to-all-start.1 = ((f32[3,256,256]{2,0,1:T(4,128)}), f32[3,256,256]{2,0,1:T(4,128)S(1)}, u32[]{:S(2)}, u32[]{:S(2)}) async-start(f32[3,256,256]{2,0,1:T(4,128)} %copy.61), calls=%async_computation.1 | async-start | bytes 2097152 | tf_op jit(solution)/shard_map/all_to_all | solution.py:69
  65.6 2.9 %copy-start.5 = (bf16[3,1024,128]{2,1,0:T(8,128)(2,1)S(1)}, bf16[3,1024,128]{2,1,0:T(8,128)(2,1)}, u32[]{:S(2)}) copy-start(bf16[3,1024,128]{2,1,0:T(8,128)(2,1)} %param.15) | copy-start | bytes 2359300
  92.4 14.8 %collective-permute-start = (f32[16,8,256]{2,0,1:T(8,128)S(1)}, f32[16,8,256]{2,0,1:T(8,128)S(1)}, u32[]{:S(2)}, u32[]{:S(2)}) collective-permute-start(f32[16,8,256]{2,0,1:T(8,128)S(1)} %slice.39), channel_id=1, source_target_pairs={{0,32},{32,64},{64,96},{96,128},{128,160},{160,192},{192,224},{224... | collective-permute-start | bytes 393224 | tf_op jit(solution)/shard_map/ppermute | solution.py:11
where the time goes:
time: 109 us; the launch traced here: 108 us
  local copies, waits for them, and re-layouts  33.3 us (31%)
  waiting for transfers between devices  30.9 us (28%)
  matrix products  22.6 us (21%)
  starting transfers between devices  18.5 us (17%)
  between operations  1.81 us (2%)
    all_to_all x1, waiting for transfers between devices, per_device(): lax.all_to_all(parts, 'sub', split_axis=1, concat_axis=0, tiled=True)  20 us
    dot_general x12, matrix products, contract(): lax.dot_general(left, right, (((0,), (0,)), ((), ())), preferred_element_...  17.7 us
    gather x9, local copies, waits for them, and re-layouts, per_device(): placed = reduced[inverse][:, inverse] * active  10.9 us
    ppermute x1, waiting for transfers between devices, shifted(): lax.ppermute(value, axis, [(i, (i + by) % peers) for i in range(peers)])  10.9 us
    all_to_all x1, starting transfers between devices, per_device(): lax.all_to_all(spread_hot, 'sub', split_axis=1, concat_axis=0, tiled=True)  9.19 us
    all_to_all x1, starting transfers between devices, per_device(): lax.all_to_all(parts, 'sub', split_axis=1, concat_axis=0, tiled=True)  7.74 us
    unnamed x25, local copies, waits for them, and re-layouts  6.59 us
    dot_general x3, local copies, waits for them, and re-layouts, contract(): lax.dot_general(left, right, (((0,), (0,)), ((), ())), preferred_element_...  4.48 us
  transfers between devices with their start and end apart: 3, of which 2 were waited for; matrix products, arithmetic and copies ran while one was open for 49% of the time, Pallas kernels for 0%

commit v1 on v0

v1 whole, which is shorter than its diff:
```python
import functools

import jax
import jax.numpy as jnp
from jax import lax
from jax.experimental import pallas as pl
from jax.experimental.pallas import tpu as pltpu
from jax.sharding import PartitionSpec as P

NBG = 16
X_CHIPS = 4
Z_RUN = 4
MESH = pl.DeviceIdType.MESH
HALVES = 2
LANES = 128


def contract(left, right):
    return lax.dot_general(left, right, (((0,), (0,)), ((), ())), preferred_element_type=jnp.float32)


def split(value):
    high = value.astype(jnp.bfloat16)
    low = (value - high.astype(jnp.float32)).astype(jnp.bfloat16)
    return high, low


def body(
    n_grp,
    n_sub,
    counts,
    codes_in,
    perms,
    mass_ii,
    mass_ib,
    mass_bb,
    modes,
    fixed,
    blocks,
    coupling,
    m_buf,
    pi_buf,
    b_buf,
    c_buf,
    f_buf,
    perm_buf,
    placed,
    rows_in,
    code_row,
    code_in,
    acc,
    staged,
    ahead_in,
    home_in,
    coup_buf,
    block_buf,
    load_sem,
    half_sem,
    out_sem,
    row_send,
    row_recv,
    code_sem,
    end_sem,
):
    slots, inner, width = mass_ib.shape
    own = width // n_sub
    grp = lax.axis_index("grp")
    sub = lax.axis_index("sub")
    run = n_sub // Z_RUN

    def mirrored(device):
        return (Z_RUN - 1 - device // run) * run + lax.rem(device, run)

    last = lax.rem(grp, X_CHIPS) == X_CHIPS - 1
    first = lax.rem(grp, X_CHIPS) == 0
    next_grp = lax.rem(grp + 1, n_grp)
    prev_grp = lax.rem(grp + n_grp - 1, n_grp)
    out_sub = jnp.where(last, mirrored(sub), sub)
    in_sub = jnp.where(first, mirrored(sub), sub)

    def loads(j):
        half = inner // HALVES
        copies = [pltpu.make_async_copy(modes.at[j], c_buf.at[j], load_sem.at[j, 0])]
        for part in range(HALVES):
            rows = pl.ds(part * half, half)
            copies.append(pltpu.make_async_copy(mass_ii.at[j, rows], m_buf.at[j, rows], half_sem.at[j, part]))
        copies.append(pltpu.make_async_copy(mass_ib.at[j], pi_buf.at[j, :, pl.ds(width, width)], load_sem.at[j, 1]))
        copies.append(pltpu.make_async_copy(mass_bb.at[j], b_buf.at[j], load_sem.at[j, 2]))
        copies.append(pltpu.make_async_copy(fixed.at[j], f_buf.at[j], load_sem.at[j, 3]))
        return copies

    for copy in loads(0):
        copy.start()
    perm_copy = pltpu.make_async_copy(perms, perm_buf, load_sem.at[0, 4])
    perm_copy.start()

    barrier = pltpu.get_barrier_semaphore()

    def greet(step, carry):
        peer = lax.rem(sub + step, n_sub)
        pl.semaphore_signal(barrier, inc=1, device_id={"sub": peer}, device_id_type=MESH)
        return carry

    lax.fori_loop(1, n_sub, greet, 0)
    pl.semaphore_signal(barrier, inc=1, device_id={"grp": next_grp, "sub": out_sub}, device_id_type=MESH)
    pl.semaphore_signal(barrier, inc=1, device_id={"grp": prev_grp, "sub": in_sub}, device_id_type=MESH)

    used = counts[0]
    lane = lax.broadcasted_iota(jnp.int32, (1, 128), 1)
    row = jnp.full((1, 128), -1, jnp.int32)
    for j in range(slots):
        row = jnp.where((lane == j) & (j < used), codes_in[j], row)
    code_row[...] = row
    code_in[0] = row

    def code_copy(step):
        peer = lax.rem(sub + step, n_sub)
        return pltpu.make_async_remote_copy(
            src_ref=code_row,
            dst_ref=code_in.at[step],
            send_sem=code_sem.at[0],
            recv_sem=code_sem.at[1],
            device_id={"sub": peer},
            device_id_type=MESH,
        )

    def rows_copy(j, step):
        peer = lax.rem(sub + step, n_sub)
        block = jnp.where(last, mirrored(peer), peer)
        return pltpu.make_async_remote_copy(
            src_ref=placed.at[j, :, pl.ds(pl.multiple_of(block * own, own), own)],
            dst_ref=rows_in.at[j, :, pl.ds(pl.multiple_of(step * own, own), own)],
            send_sem=row_send.at[j],
            recv_sem=row_recv.at[j],
            device_id={"sub": peer},
            device_id_type=MESH,
        )

    perm_copy.wait()
    row_of = lax.broadcasted_iota(jnp.int32, (width, width), 0)

    def slot(j, carry):
        ready = loads(j)
        half = inner // HALVES
        ready[0].wait()
        for part in range(HALVES):
            ready[1 + part].wait()
            if part == HALVES - 1:

                @pl.when(j + 1 < slots)
                def _():
                    for copy in loads(j + 1):
                        copy.start()

            rows = pl.ds(part * half, half)
            pi_buf[j, rows, pl.ds(0, width)] = jnp.dot(
                m_buf[j, rows], c_buf[j], preferred_element_type=jnp.float32
            ).astype(jnp.bfloat16)
        ready[1 + HALVES].wait()
        ready[2 + HALVES].wait()
        both = contract(c_buf[j], pi_buf[j])
        cross = both[:, width:]
        reduced = both[:, :width] + cross + cross.T + b_buf[j].astype(jnp.float32)
        hot = (row_of == perm_buf[pl.ds(j, 1), :]).astype(jnp.float32).astype(jnp.bfloat16)
        high, low = split(reduced)
        moved_high = jnp.dot(hot, high, preferred_element_type=jnp.float32).astype(jnp.bfloat16)
        moved_low = jnp.dot(hot, low, preferred_element_type=jnp.float32).astype(jnp.bfloat16)
        across = (((1,), (1,)), ((), ()))
        moved = lax.dot_general(
            moved_high, hot, across, preferred_element_type=jnp.float32
        ) + lax.dot_general(moved_low, hot, across, preferred_element_type=jnp.float32)
        for side in range(width // LANES):
            placed[j, side] = moved[:, side * LANES : (side + 1) * LANES]

        @pl.when(j == 0)
        def _():
            pl.semaphore_wait(barrier, n_sub + 1)
            lax.fori_loop(1, n_sub, lambda step, c: (code_copy(step).start(), c)[1], 0)

        lax.fori_loop(1, n_sub, lambda step, c: (rows_copy(j, step).start(), c)[1], 0)
        mine = pl.ds(pl.multiple_of(out_sub * own, own), own)
        rows_in[j, :, pl.ds(0, own)] = placed[j, :, mine]

        ready[3 + HALVES].wait()
        pair = contract(f_buf[j], pi_buf[j])
        coupled = pair[:, :width] + pair[:, width:]
        coup_buf[j] = jnp.where(j < used, coupled, 0.0)
        pltpu.make_async_copy(coup_buf.at[j], coupling.at[j], out_sem.at[j]).start()
        return carry

    lax.fori_loop(0, slots, slot, 0)

    others = pltpu.make_async_remote_copy(
        src_ref=code_in.at[pl.ds(1, n_sub - 1)],
        dst_ref=code_in.at[pl.ds(1, n_sub - 1)],
        send_sem=code_sem.at[0],
        recv_sem=code_sem.at[1],
        device_id={"sub": sub},
        device_id_type=MESH,
    )
    others.wait_send()
    others.wait_recv()
    code_all = code_in[...].reshape(n_sub, 128)
    target = lax.broadcasted_iota(jnp.int32, (n_sub, 2 * NBG), 1)
    for j in range(slots):
        rest = pl.ds(own, width - own)
        arrived = pltpu.make_async_remote_copy(
            src_ref=rows_in.at[j, :, rest],
            dst_ref=rows_in.at[j, :, rest],
            send_sem=row_send.at[j],
            recv_sem=row_recv.at[j],
            device_id={"sub": sub},
            device_id_type=MESH,
        )
        arrived.wait_recv()
        arrived.wait_send()
        hot = (code_all[:, j : j + 1] == target).astype(jnp.float32).astype(jnp.bfloat16)
        hot = jnp.concatenate([hot, hot], axis=0)
        for r in range(own):
            for side in range(width // LANES):
                high, low = split(rows_in[j, side, pl.ds(r, n_sub, stride=own), :])
                part = contract(hot, jnp.concatenate([high, low], axis=0))
                if j > 0:
                    part = part + acc[r, side]
                if j < slots - 1:
                    acc[r, side] = part
                else:
                    staged[side, pl.ds(r, 2 * NBG, stride=own), :] = part

    size = NBG * own
    ahead = pltpu.make_async_remote_copy(
        src_ref=staged.at[:, pl.ds(size, size)],
        dst_ref=ahead_in,
        send_sem=end_sem.at[0],
        recv_sem=end_sem.at[1],
        device_id={"grp": next_grp, "sub": out_sub},
        device_id_type=MESH,
    )
    ahead.start()
    home = pltpu.make_async_remote_copy(
        src_ref=staged.at[:, pl.ds(0, size)],
        dst_ref=home_in,
        send_sem=end_sem.at[2],
        recv_sem=end_sem.at[3],
        device_id={"sub": out_sub},
        device_id_type=MESH,
    )

    @pl.when(last)
    def _():
        home.start()
        home.wait()

    @pl.when(jnp.logical_not(last))
    def _():
        home_in[...] = staged[:, pl.ds(0, size)]

    ahead.wait()
    for side in range(width // LANES):
        block_buf[:, :, pl.ds(side * LANES, LANES)] = (home_in[side] + ahead_in[side]).reshape(NBG, own, LANES)
    out = pltpu.make_async_copy(block_buf, blocks, out_sem.at[slots])
    out.start()
    for j in range(slots):
        pltpu.make_async_copy(coup_buf.at[j], coupling.at[j], out_sem.at[j]).wait()
    out.wait()


def solution(mesh):
    n_grp, n_sub = mesh.shape["grp"], mesh.shape["sub"]

    def per_device(counts, block_map, perms, mass_ii, mass_ib, mass_bb, modes, fixed):
        slots, inner, width = mass_ib.shape
        k = fixed.shape[2]
        own = width // n_sub
        anywhere = pl.BlockSpec(memory_space=pl.ANY)
        smem = pl.BlockSpec(memory_space=pltpu.SMEM)
        flops = 2 * slots * inner * width * (inner + 2 * width + 2 * k)
        return pl.pallas_call(
            functools.partial(body, n_grp, n_sub),
            out_shape=(
                jax.ShapeDtypeStruct((NBG, own, width), jnp.float32),
                jax.ShapeDtypeStruct((slots, k, width), jnp.float32),
            ),
            in_specs=[smem, smem] + [anywhere] * 6,
            out_specs=(anywhere, anywhere),
            scratch_shapes=[
                pltpu.VMEM((slots, inner, inner), jnp.bfloat16),
                pltpu.VMEM((slots, inner, 2 * width), jnp.bfloat16),
                pltpu.VMEM((slots, width, width), jnp.bfloat16),
                pltpu.VMEM((slots, inner, width), jnp.bfloat16),
                pltpu.VMEM((slots, inner, k), jnp.bfloat16),
                pltpu.VMEM((slots, width), jnp.int32),
                pltpu.VMEM((slots, width // LANES, width, LANES), jnp.float32),
                pltpu.VMEM((slots, width // LANES, width, LANES), jnp.float32),
                pltpu.VMEM((1, 128), jnp.int32),
                pltpu.VMEM((n_sub, 1, 128), jnp.int32),
                pltpu.VMEM((own, width // LANES, 2 * NBG, LANES), jnp.float32),
                pltpu.VMEM((width // LANES, 2 * NBG * own, LANES), jnp.float32),
                pltpu.VMEM((width // LANES, NBG * own, LANES), jnp.float32),
                pltpu.VMEM((width // LANES, NBG * own, LANES), jnp.float32),
                pltpu.VMEM((slots, k, width), jnp.float32),
                pltpu.VMEM((NBG, own, width), jnp.float32),
                pltpu.SemaphoreType.DMA((slots, 5)),
                pltpu.SemaphoreType.DMA((slots, HALVES)),
                pltpu.SemaphoreType.DMA((slots + 1,)),
                pltpu.SemaphoreType.DMA((slots,)),
                pltpu.SemaphoreType.DMA((slots,)),
                pltpu.SemaphoreType.DMA((2,)),
                pltpu.SemaphoreType.DMA((4,)),
            ],
            compiler_params=pltpu.CompilerParams(
                collective_id=0, has_side_effects=True, vmem_limit_bytes=60 * 1024 * 1024
            ),
            cost_estimate=pl.CostEstimate(flops=flops, bytes_accessed=12 << 20, transcendentals=0),
            name="reduce_assemble",
        )(counts, block_map, perms, mass_ii, mass_ib, mass_bb, modes, fixed)

    shared = ("grp", "sub")
    return jax.shard_map(
        per_device,
        mesh=mesh,
        in_specs=(P(shared), P(shared), P(shared, None)) + (P(shared, None, None),) * 5,
        out_specs=(P("grp", "sub", None), P(shared, None, None)),
        check_vma=False,
    )
```

time: 109 us -> 46.6 us (0.43)
  the two profiles are of different devices: /device:TPU:8 before, /device:TPU:1 now
where the time goes in v1:
time: 46.6 us; the launch traced here: 46.4 us
  Pallas kernels  41.8 us (90%)
  local copies, waits for them, and re-layouts  3.33 us (7%)
  between operations  1.29 us (3%)
    pallas_call x1, Pallas kernels, per_device(): pl.pallas_call(functools.partial(body, n_grp, n_sub), out_shape=(jax.Shap...  41.8 us
    unnamed x2, local copies, waits for them, and re-layouts  3.33 us

profile of v1, /device:TPU:1, one launch (start us, length us, event | category | flops | bytes accessed | tf_op | source)
XLA Modules:
  0.0 46.4 jit_solution(5165788212863612030)
XLA Ops:
  1.3 41.8 %reduce_assemble.1 = (f32[16,8,256]{2,1,0:T(8,128)}, f32[3,128,256]{2,1,0:T(8,128)}) custom-call(s32[1]{0:T(128)S(6)} %copy.12.counts, s32[3]{0:T(128)} %codes_in.1, s32[3,256]{1,0:T(4,128)} %perms.1, bf16[3,1024,1024]{2,1,0:T(8,128)(2,1)} %mass_ii.1, bf16[3,1024,256]{2,1,0:T(8,128)(2,1)} %mass_ib.1, bf16[3,256,256]{2,1,0:T(8,128)(2,1)} %mass_bb.1, ...), custom_call_target="tpu_custom_call" | custom-call | flops 2818572288 | bytes 12582912 | tf_op jit(solution)/shard_map/reduce_assemble/pallas_call | solution.py:278
  43.1 1.6 %copy.13 = f32[16,8,256]{2,1,0:T(8,128)} copy(f32[16,8,256]{2,1,0:T(8,128)} %get-tuple-element.4) | data formatting | bytes 262144
  44.7 1.8 %copy.14 = f32[3,128,256]{2,1,0:T(8,128)} copy(f32[3,128,256]{2,1,0:T(8,128)} %get-tuple-element.5) | data formatting | bytes 786432

commit v2 on v1

v2 whole, which is shorter than its diff:
```python
import functools

import jax
import jax.numpy as jnp
from jax import lax
from jax.experimental import pallas as pl
from jax.experimental.pallas import tpu as pltpu
from jax.sharding import PartitionSpec as P

NBG = 16
X_CHIPS = 4
Z_RUN = 4
MESH = pl.DeviceIdType.MESH
PARTS = 4
SIDES = 2
LANES = 128


def contract(left, right):
    return lax.dot_general(left, right, (((0,), (0,)), ((), ())), preferred_element_type=jnp.float32)


def split(value):
    high = value.astype(jnp.bfloat16)
    low = (value - high.astype(jnp.float32)).astype(jnp.bfloat16)
    return high, low


def body(
    n_grp,
    n_sub,
    counts,
    codes_any,
    perms,
    mass_ii,
    mass_ib,
    mass_bb,
    modes,
    fixed,
    blocks,
    coupling,
    m_buf,
    pi_buf,
    b_buf,
    c_buf,
    f_buf,
    perm_buf,
    placed,
    rows_in,
    code_row,
    code_in,
    hot_all,
    staged,
    ahead_in,
    home_in,
    relay_in,
    load_sem,
    part_sem,
    codes_in,
    row_send,
    row_recv,
    code_sem,
    end_sem,
):
    slots, inner, width = mass_ib.shape
    own = width // n_sub
    grp = lax.axis_index("grp")
    sub = lax.axis_index("sub")
    run = n_sub // Z_RUN

    def mirrored(device):
        return (Z_RUN - 1 - device // run) * run + lax.rem(device, run)

    last = lax.rem(grp, X_CHIPS) == X_CHIPS - 1
    first = lax.rem(grp, X_CHIPS) == 0
    next_grp = lax.rem(grp + 1, n_grp)
    prev_grp = lax.rem(grp + n_grp - 1, n_grp)
    out_sub = jnp.where(last, mirrored(sub), sub)
    in_sub = jnp.where(first, mirrored(sub), sub)
    far_grp = lax.rem(grp + X_CHIPS, n_grp)

    def loads(j):
        step = inner // PARTS
        copies = [pltpu.make_async_copy(modes.at[j], c_buf.at[j], load_sem.at[j, 0])]
        for part in range(PARTS):
            rows = pl.ds(part * step, step)
            copies.append(pltpu.make_async_copy(mass_ii.at[j, rows], m_buf.at[j, rows], part_sem.at[j, part]))
        copies.append(pltpu.make_async_copy(mass_ib.at[j], pi_buf.at[j, :, pl.ds(width, width)], load_sem.at[j, 1]))
        copies.append(pltpu.make_async_copy(mass_bb.at[j], b_buf.at[j], load_sem.at[j, 2]))
        copies.append(pltpu.make_async_copy(fixed.at[j], f_buf.at[j], load_sem.at[j, 3]))
        return copies

    for copy in loads(0):
        copy.start()
    small = (
        pltpu.make_async_copy(perms, perm_buf, load_sem.at[0, 4]),
        pltpu.make_async_copy(codes_any, codes_in, load_sem.at[2, 4]),
    )
    for copy in small:
        copy.start()

    barrier = pltpu.get_barrier_semaphore()

    def greet(step, carry):
        peer = lax.rem(sub + step, n_sub)
        pl.semaphore_signal(barrier, inc=1, device_id={"sub": peer}, device_id_type=MESH)
        return carry

    lax.fori_loop(1, n_sub, greet, 0)
    pl.semaphore_signal(barrier, inc=1, device_id={"grp": next_grp, "sub": out_sub}, device_id_type=MESH)
    pl.semaphore_signal(barrier, inc=1, device_id={"grp": prev_grp, "sub": in_sub}, device_id_type=MESH)

    @pl.when(last)
    def _():
        pl.semaphore_signal(barrier, inc=1, device_id={"grp": grp - (X_CHIPS - 1)}, device_id_type=MESH)

    @pl.when(first)
    def _():
        pl.semaphore_signal(barrier, inc=1, device_id={"grp": grp + (X_CHIPS - 1)}, device_id_type=MESH)
        pl.semaphore_signal(barrier, inc=1, device_id={"grp": far_grp}, device_id_type=MESH)

    greeted = n_sub + 1 + jnp.where(last, 1, 0) + jnp.where(first, 2, 0)

    for copy in small:
        copy.wait()
    used = counts[0]
    lane = lax.broadcasted_iota(jnp.int32, (1, 128), 1)
    row = jnp.full((1, 128), -1, jnp.int32)
    for j in range(slots):
        row = jnp.where((lane == j) & (j < used), codes_in[j], row)
    code_row[...] = row
    code_in[0] = row

    def code_copy(step):
        peer = lax.rem(sub + step, n_sub)
        return pltpu.make_async_remote_copy(
            src_ref=code_row,
            dst_ref=code_in.at[step],
            send_sem=code_sem.at[0],
            recv_sem=code_sem.at[1],
            device_id={"sub": peer},
            device_id_type=MESH,
        )

    def left_copy(j, step):
        peer = lax.rem(sub + step, n_sub)
        return pltpu.make_async_remote_copy(
            src_ref=placed.at[0, j, pl.ds(pl.multiple_of(peer * own, own), own)],
            dst_ref=rows_in.at[0, j, pl.ds(pl.multiple_of(step * own, own), own)],
            send_sem=row_send.at[j],
            recv_sem=row_recv.at[j],
            device_id={"sub": peer},
            device_id_type=MESH,
        )

    def right_copy(step):
        peer = lax.rem(sub + step, n_sub)
        block = jnp.where(last, mirrored(peer), peer)
        return pltpu.make_async_remote_copy(
            src_ref=placed.at[1, :, pl.ds(pl.multiple_of(block * own, own), own)],
            dst_ref=rows_in.at[1, :, pl.ds(pl.multiple_of(step * own, own), own)],
            send_sem=row_send.at[slots],
            recv_sem=row_recv.at[slots],
            device_id={"sub": peer},
            device_id_type=MESH,
        )

    row_of = lax.broadcasted_iota(jnp.int32, (width, width), 0)

    def slot(j, carry):
        ready = loads(j)
        step = inner // PARTS
        ready[0].wait()
        for part in range(PARTS):
            ready[1 + part].wait()
            if part == PARTS - 1:

                @pl.when(j + 1 < slots)
                def _():
                    for copy in loads(j + 1):
                        copy.start()

            rows = pl.ds(part * step, step)
            pi_buf[j, rows, pl.ds(0, width)] = jnp.dot(
                m_buf[j, rows], c_buf[j], preferred_element_type=jnp.float32
            ).astype(jnp.bfloat16)
        ready[1 + PARTS].wait()
        ready[2 + PARTS].wait()
        both = contract(c_buf[j], pi_buf[j])
        cross = both[:, width:]
        reduced = both[:, :width] + cross + cross.T + b_buf[j].astype(jnp.float32)
        hot = (row_of == perm_buf[pl.ds(j, 1), :]).astype(jnp.float32).astype(jnp.bfloat16)
        high, low = split(reduced)
        moved_high = jnp.dot(hot, high, preferred_element_type=jnp.float32).astype(jnp.bfloat16)
        moved_low = jnp.dot(hot, low, preferred_element_type=jnp.float32).astype(jnp.bfloat16)
        across = (((1,), (1,)), ((), ()))
        moved = lax.dot_general(
            moved_high, hot, across, preferred_element_type=jnp.float32
        ) + lax.dot_general(moved_low, hot, across, preferred_element_type=jnp.float32)
        for side in range(SIDES):
            placed[side, j] = moved[:, side * LANES : (side + 1) * LANES]

        @pl.when(j == 0)
        def _():
            pl.semaphore_wait(barrier, greeted)
            lax.fori_loop(1, n_sub, lambda step, c: (code_copy(step).start(), c)[1], 0)

        lax.fori_loop(1, n_sub, lambda step, c: (left_copy(j, step).start(), c)[1], 0)
        return carry

    lax.fori_loop(0, slots, slot, 0)

    lax.fori_loop(1, n_sub, lambda step, c: (right_copy(step).start(), c)[1], 0)
    rows_in[0, :, pl.ds(0, own)] = placed[0, :, pl.ds(pl.multiple_of(sub * own, own), own)]
    rows_in[1, :, pl.ds(0, own)] = placed[1, :, pl.ds(pl.multiple_of(out_sub * own, own), own)]

    def couple(j, carry):
        loads(j)[3 + PARTS].wait()
        pair = contract(f_buf[j], pi_buf[j])
        coupling[j] = jnp.where(j < used, pair[:, :width] + pair[:, width:], 0.0)
        return carry

    lax.fori_loop(0, slots, couple, 0)

    others = pltpu.make_async_remote_copy(
        src_ref=code_in.at[pl.ds(1, n_sub - 1)],
        dst_ref=code_in.at[pl.ds(1, n_sub - 1)],
        send_sem=code_sem.at[0],
        recv_sem=code_sem.at[1],
        device_id={"sub": sub},
        device_id_type=MESH,
    )
    others.wait_send()
    others.wait_recv()
    code_all = code_in[...].reshape(n_sub, 128)
    target = lax.broadcasted_iota(jnp.int32, (n_sub, 2 * NBG), 1)
    hot = jnp.concatenate([(code_all[:, j : j + 1] == target).astype(jnp.float32) for j in range(slots)] * 2, axis=0)
    hot_all[...] = hot.T.astype(jnp.bfloat16)

    def arrived(side, j, sem):
        refs = rows_in.at[side, j, pl.ds(own, width - own)]
        copy = pltpu.make_async_remote_copy(
            src_ref=refs,
            dst_ref=refs,
            send_sem=row_send.at[sem],
            recv_sem=row_recv.at[sem],
            device_id={"sub": sub},
            device_id_type=MESH,
        )
        copy.wait_recv()
        copy.wait_send()

    def assemble(side):
        for r in range(0, own, 2):
            terms = []
            for q in (r, r + 1):
                pieces = [split(rows_in[side, j, pl.ds(q, n_sub, stride=own), :]) for j in range(slots)]
                terms.append(jnp.concatenate([p[0] for p in pieces] + [p[1] for p in pieces], axis=0))
            sums = jnp.dot(hot_all[...], jnp.concatenate(terms, axis=1), preferred_element_type=jnp.float32)
            for q in range(2):
                staged[side, pl.ds(r + q, 2 * NBG, stride=own), :] = sums[:, q * LANES : (q + 1) * LANES]

    size = NBG * own

    def end_copy(src, dst, sent, landed, device):
        return pltpu.make_async_remote_copy(
            src_ref=src,
            dst_ref=dst,
            send_sem=end_sem.at[0, sent],
            recv_sem=end_sem.at[1, landed],
            device_id=device,
            device_id_type=MESH,
        )

    def write(side):
        blocks[:, :, pl.ds(side * LANES, LANES)] = (home_in[side] + ahead_in[side]).reshape(NBG, own, LANES)

    def ahead_of(side):
        return staged.at[side, pl.ds(size, size)]

    for j in range(slots):
        arrived(0, j, j)
    assemble(0)
    straight = end_copy(ahead_of(0), ahead_in.at[0], 0, 0, {"grp": next_grp})
    aside = end_copy(ahead_of(0), relay_in, 1, 1, {"grp": grp - (X_CHIPS - 1)})
    onward = end_copy(relay_in, ahead_in.at[0], 4, 0, {"grp": far_grp})

    @pl.when(last)
    def _():
        aside.start()

    @pl.when(jnp.logical_not(last))
    def _():
        straight.start()

    home_in[0] = staged[0, pl.ds(0, size)]

    @pl.when(first)
    def _():
        aside.wait_recv()
        onward.start()

    arrived(1, slice(None), slots)
    assemble(1)
    ahead = end_copy(ahead_of(1), ahead_in.at[1], 2, 2, {"grp": next_grp, "sub": out_sub})
    home = end_copy(staged.at[1, pl.ds(0, size)], home_in.at[1], 3, 3, {"sub": out_sub})
    ahead.start()

    @pl.when(last)
    def _():
        home.start()

    @pl.when(jnp.logical_not(last))
    def _():
        home_in[1] = staged[1, pl.ds(0, size)]

    straight.wait_recv()
    write(0)

    @pl.when(last)
    def _():
        aside.wait_send()
        home.wait()

    @pl.when(jnp.logical_not(last))
    def _():
        straight.wait_send()

    @pl.when(first)
    def _():
        onward.wait_send()

    ahead.wait()
    write(1)


def solution(mesh):
    n_grp, n_sub = mesh.shape["grp"], mesh.shape["sub"]

    def per_device(counts, block_map, perms, mass_ii, mass_ib, mass_bb, modes, fixed):
        slots, inner, width = mass_ib.shape
        k = fixed.shape[2]
        operands = (block_map, perms, mass_ii, mass_ib, mass_bb, modes, fixed)
        own = width // n_sub
        far = pl.BlockSpec(memory_space=pltpu.HBM)
        near = pl.BlockSpec(memory_space=pltpu.VMEM)
        flops = 2 * slots * inner * width * (inner + 2 * width + 2 * k)
        return pl.pallas_call(
            functools.partial(body, n_grp, n_sub),
            out_shape=(
                jax.ShapeDtypeStruct((NBG, own, width), jnp.float32),
                jax.ShapeDtypeStruct((slots, k, width), jnp.float32),
            ),
            in_specs=[pl.BlockSpec(memory_space=pltpu.SMEM)] + [far] * 7,
            out_specs=(near, near),
            scratch_shapes=[
                pltpu.VMEM((slots, inner, inner), jnp.bfloat16),
                pltpu.VMEM((slots, inner, 2 * width), jnp.bfloat16),
                pltpu.VMEM((slots, width, width), jnp.bfloat16),
                pltpu.VMEM((slots, inner, width), jnp.bfloat16),
                pltpu.VMEM((slots, inner, k), jnp.bfloat16),
                pltpu.VMEM((slots, width), jnp.int32),
                pltpu.VMEM((SIDES, slots, width, LANES), jnp.float32),
                pltpu.VMEM((SIDES, slots, width, LANES), jnp.float32),
                pltpu.VMEM((1, 128), jnp.int32),
                pltpu.VMEM((n_sub, 1, 128), jnp.int32),
                pltpu.VMEM((2 * NBG, 2 * slots * n_sub), jnp.bfloat16),
                pltpu.VMEM((SIDES, 2 * NBG * own, LANES), jnp.float32),
                pltpu.VMEM((SIDES, NBG * own, LANES), jnp.float32),
                pltpu.VMEM((SIDES, NBG * own, LANES), jnp.float32),
                pltpu.VMEM((NBG * own, LANES), jnp.float32),
                pltpu.SemaphoreType.DMA((slots, 5)),
                pltpu.SemaphoreType.DMA((slots, PARTS)),
                pltpu.SMEM((slots,), jnp.int32),
                pltpu.SemaphoreType.DMA((slots + 1,)),
                pltpu.SemaphoreType.DMA((slots + 1,)),
                pltpu.SemaphoreType.DMA((2,)),
                pltpu.SemaphoreType.DMA((2, 5)),
            ],
            compiler_params=pltpu.CompilerParams(
                collective_id=0, has_side_effects=True, vmem_limit_bytes=24 * 1024 * 1024
            ),
            cost_estimate=pl.CostEstimate(flops=flops, bytes_accessed=12 << 20, transcendentals=0),
            name="reduce_assemble",
        )(counts, *(pltpu.with_memory_space_constraint(a, pltpu.HBM) for a in operands))

    shared = ("grp", "sub")
    return jax.shard_map(
        per_device,
        mesh=mesh,
        in_specs=(P(shared), P(shared), P(shared, None)) + (P(shared, None, None),) * 5,
        out_specs=(P("grp", "sub", None), P(shared, None, None)),
        check_vma=False,
    )
```

time: 46.6 us -> 40 us (0.86)
  Pallas kernels: 41.8 us -> 37.2 us
  local copies, waits for them, and re-layouts: 3.33 us -> 1.4 us
    pallas_call x1, Pallas kernels: 41.8 us -> 37.2 us  [per_device(): pl.pallas_call(functools.partial(body, n_grp, n_sub), out_shape=(jax.Shap...]
    unnamed x2, local copies, waits for them, and re-layouts: 3.33 us -> 1.4 us
where the time goes in v2:
time: 40 us; the launch traced here: 39.9 us
  Pallas kernels  37.2 us (93%)
  local copies, waits for them, and re-layouts  1.4 us (4%)
  between operations  1.29 us (3%)
    pallas_call x1, Pallas kernels, per_device(): pl.pallas_call(functools.partial(body, n_grp, n_sub), out_shape=(jax.Shap...  37.2 us
    unnamed x2, local copies, waits for them, and re-layouts  1.4 us

profile of v2, /device:TPU:1, one launch (start us, length us, event | category | flops | bytes accessed | tf_op | source)
XLA Modules:
  0.0 39.9 jit_solution(14859793704578182448)
XLA Ops:
  1.3 37.2 %reduce_assemble.1 = (f32[16,8,256]{2,1,0:T(8,128)S(1)}, f32[3,128,256]{2,1,0:T(8,128)S(1)}) custom-call(s32[1]{0:T(128)S(6)} %copy.12.counts, s32[3]{0:T(128)} %codes_any.1, s32[3,256]{1,0:T(4,128)} %perms.1, bf16[3,1024,1024]{2,1,0:T(8,128)(2,1)} %mass_ii.1, bf16[3,1024,256]{2,1,0:T(8,128)(2,1)} %mass_ib.1, bf16[3,256,256]{2,1,0:T(8,128)(2,1)} %mass_bb.1, ...), custom_call_target="tpu_custom_call" | custom-call | flops 2818572288 | bytes 12582912 | tf_op jit(solution)/shard_map/reduce_assemble/pallas_call | solution.py:348
  38.5 0.7 %copy.13 = f32[16,8,256]{2,1,0:T(8,128)} copy(f32[16,8,256]{2,1,0:T(8,128)S(1)} %get-tuple-element.4) | data formatting | bytes 262144
  39.2 0.7 %copy.14 = f32[3,128,256]{2,1,0:T(8,128)} copy(f32[3,128,256]{2,1,0:T(8,128)S(1)} %get-tuple-element.5) | data formatting | bytes 786432

commit v3 on v2

--- a/solution.py
+++ b/solution.py
@@ -11,7 +11,7 @@
 X_CHIPS = 4
 Z_RUN = 4
 MESH = pl.DeviceIdType.MESH
-PARTS = 4
+PARTS = 2
 SIDES = 2
 LANES = 128
 
@@ -79,25 +79,32 @@
     in_sub = jnp.where(first, mirrored(sub), sub)
     far_grp = lax.rem(grp + X_CHIPS, n_grp)
 
-    def loads(j):
-        step = inner // PARTS
-        copies = [pltpu.make_async_copy(modes.at[j], c_buf.at[j], load_sem.at[j, 0])]
-        for part in range(PARTS):
-            rows = pl.ds(part * step, step)
-            copies.append(pltpu.make_async_copy(mass_ii.at[j, rows], m_buf.at[j, rows], part_sem.at[j, part]))
-        copies.append(pltpu.make_async_copy(mass_ib.at[j], pi_buf.at[j, :, pl.ds(width, width)], load_sem.at[j, 1]))
-        copies.append(pltpu.make_async_copy(mass_bb.at[j], b_buf.at[j], load_sem.at[j, 2]))
-        copies.append(pltpu.make_async_copy(fixed.at[j], f_buf.at[j], load_sem.at[j, 3]))
-        return copies
-
-    for copy in loads(0):
-        copy.start()
+    def load(j, at):
+        pairs = (
+            (modes.at[j], c_buf.at[j]),
+            (mass_ib.at[j], pi_buf.at[j, :, pl.ds(width, width)]),
+            (mass_bb.at[j], b_buf.at[j]),
+            (fixed.at[j], f_buf.at[j]),
+        )
+        return pltpu.make_async_copy(*pairs[at], load_sem.at[j, at])
+
+    def load_part(j, part):
+        rows = pl.ds(pl.multiple_of(part * (inner // PARTS), inner // PARTS), inner // PARTS)
+        return pltpu.make_async_copy(mass_ii.at[j, rows], m_buf.at[j, rows], part_sem.at[j, part])
+
+    def start_loads(j):
+        load(j, 0).start()
+        lax.fori_loop(0, PARTS, lambda part, c: (load_part(j, part).start(), c)[1], 0)
+        for at in (1, 2, 3):
+            load(j, at).start()
+
     small = (
+        pltpu.make_async_copy(codes_any, codes_in, load_sem.at[2, 4]),
         pltpu.make_async_copy(perms, perm_buf, load_sem.at[0, 4]),
-        pltpu.make_async_copy(codes_any, codes_in, load_sem.at[2, 4]),
     )
-    for copy in small:
-        copy.start()
+    small[1].start()
+    start_loads(0)
+    small[0].start()
 
     barrier = pltpu.get_barrier_semaphore()
 
@@ -121,15 +128,7 @@
 
     greeted = n_sub + 1 + jnp.where(last, 1, 0) + jnp.where(first, 2, 0)
 
-    for copy in small:
-        copy.wait()
     used = counts[0]
-    lane = lax.broadcasted_iota(jnp.int32, (1, 128), 1)
-    row = jnp.full((1, 128), -1, jnp.int32)
-    for j in range(slots):
-        row = jnp.where((lane == j) & (j < used), codes_in[j], row)
-    code_row[...] = row
-    code_in[0] = row
 
     def code_copy(step):
         peer = lax.rem(sub + step, n_sub)
@@ -165,27 +164,28 @@
             device_id_type=MESH,
         )
 
+    small[1].wait()
     row_of = lax.broadcasted_iota(jnp.int32, (width, width), 0)
 
     def slot(j, carry):
-        ready = loads(j)
-        step = inner // PARTS
-        ready[0].wait()
-        for part in range(PARTS):
-            ready[1 + part].wait()
-            if part == PARTS - 1:
-
-                @pl.when(j + 1 < slots)
-                def _():
-                    for copy in loads(j + 1):
-                        copy.start()
-
-            rows = pl.ds(part * step, step)
+        load(j, 0).wait()
+
+        def product(part, c):
+            load_part(j, part).wait()
+
+            @pl.when((part == 0) & (j + 1 < slots))
+            def _():
+                start_loads(j + 1)
+
+            rows = pl.ds(pl.multiple_of(part * (inner // PARTS), inner // PARTS), inner // PARTS)
             pi_buf[j, rows, pl.ds(0, width)] = jnp.dot(
                 m_buf[j, rows], c_buf[j], preferred_element_type=jnp.float32
             ).astype(jnp.bfloat16)
-        ready[1 + PARTS].wait()
-        ready[2 + PARTS].wait()
+            return c
+
+        lax.fori_loop(0, PARTS, product, 0)
+        load(j, 1).wait()
+        load(j, 2).wait()
         both = contract(c_buf[j], pi_buf[j])
         cross = both[:, width:]
         reduced = both[:, :width] + cross + cross.T + b_buf[j].astype(jnp.float32)
@@ -202,6 +202,14 @@
 
         @pl.when(j == 0)
         def _():
+            small[0].wait()
+            lane = lax.broadcasted_iota(jnp.int32, (1, 128), 1)
+            row = jnp.full((1, 128), -1, jnp.int32)
+            for j in range(slots):
+                row = jnp.where((lane == j) & (j < used), codes_in[j], row)
+            code_row[...] = row
+            code_in[0] = row
+
             pl.semaphore_wait(barrier, greeted)
             lax.fori_loop(1, n_sub, lambda step, c: (code_copy(step).start(), c)[1], 0)
 
@@ -215,7 +223,7 @@
     rows_in[1, :, pl.ds(0, own)] = placed[1, :, pl.ds(pl.multiple_of(out_sub * own, own), own)]
 
     def couple(j, carry):
-        loads(j)[3 + PARTS].wait()
+        load(j, 3).wait()
         pair = contract(f_buf[j], pi_buf[j])
         coupling[j] = jnp.where(j < used, pair[:, :width] + pair[:, width:], 0.0)
         return carry
@@ -334,6 +342,17 @@
     write(1)
 
 
+def finish(blocks_in, coupling_in, blocks, coupling, sems):
+    copies = (
+        pltpu.make_async_copy(coupling_in, coupling, sems.at[0]),
+        pltpu.make_async_copy(blocks_in, blocks, sems.at[1]),
+    )
+    for copy in copies:
+        copy.start()
+    for copy in copies:
+        copy.wait()
+
+
 def solution(mesh):
     n_grp, n_sub = mesh.shape["grp"], mesh.shape["sub"]
 
@@ -345,12 +364,13 @@
         far = pl.BlockSpec(memory_space=pltpu.HBM)
         near = pl.BlockSpec(memory_space=pltpu.VMEM)
         flops = 2 * slots * inner * width * (inner + 2 * width + 2 * k)
-        return pl.pallas_call(
+        shapes = (
+            jax.ShapeDtypeStruct((NBG, own, width), jnp.float32),
+            jax.ShapeDtypeStruct((slots, k, width), jnp.float32),
+        )
+        made = pl.pallas_call(
             functools.partial(body, n_grp, n_sub),
-            out_shape=(
-                jax.ShapeDtypeStruct((NBG, own, width), jnp.float32),
-                jax.ShapeDtypeStruct((slots, k, width), jnp.float32),
-            ),
+            out_shape=shapes,
             in_specs=[pl.BlockSpec(memory_space=pltpu.SMEM)] + [far] * 7,
             out_specs=(near, near),
             scratch_shapes=[
@@ -383,6 +403,15 @@
             cost_estimate=pl.CostEstimate(flops=flops, bytes_accessed=12 << 20, transcendentals=0),
             name="reduce_assemble",
         )(counts, *(pltpu.with_memory_space_constraint(a, pltpu.HBM) for a in operands))
+        return pl.pallas_call(
+            finish,
+            out_shape=shapes,
+            in_specs=[near] * 2,
+            out_specs=(pl.BlockSpec(memory_space=pl.ANY),) * 2,
+            scratch_shapes=[pltpu.SemaphoreType.DMA((2,))],
+            compiler_params=pltpu.CompilerParams(vmem_limit_bytes=4 * 1024 * 1024),
+            name="finish",
+        )(*made)
 
     shared = ("grp", "sub")
     return jax.shard_map(

time: 40 us -> 38.2 us (0.955)
  local copies, waits for them, and re-layouts: 1.4 us -> 0 us
  Pallas kernels: 37.2 us -> 36.8 us
    unnamed x2 -> x0, local copies, waits for them, and re-layouts: 1.4 us -> none
    pallas_call x1 -> x2, Pallas kernels: 37.2 us -> 36.8 us  [the longest x1 36 us: per_device(): pl.pallas_call(functools.partial(body, n_grp, n_sub), out_shape=shapes, i...]
where the time goes in v3:
time: 38.2 us; the launch traced here: 38.1 us
  Pallas kernels  36.8 us (96%)
  between operations  1.29 us (3%)
    pallas_call x1, Pallas kernels, per_device(): pl.pallas_call(functools.partial(body, n_grp, n_sub), out_shape=shapes, i...  36 us
    pallas_call x1, Pallas kernels, per_device(): pl.pallas_call(finish, out_shape=shapes, in_specs=[near] * 2, out_specs=(...  0.8 us

profile of v3, /device:TPU:1, one launch (start us, length us, event | category | flops | bytes accessed | tf_op | source)
XLA Modules:
  0.0 38.1 jit_solution(2712743198549505677)
XLA Ops:
  1.3 36.0 %reduce_assemble.1 = (f32[16,8,256]{2,1,0:T(8,128)S(1)}, f32[3,128,256]{2,1,0:T(8,128)S(1)}) custom-call(s32[1]{0:T(128)S(6)} %copy.10.counts, s32[3]{0:T(128)} %codes_any.1, s32[3,256]{1,0:T(4,128)} %perms.1, bf16[3,1024,1024]{2,1,0:T(8,128)(2,1)} %mass_ii.1, bf16[3,1024,256]{2,1,0:T(8,128)(2,1)} %mass_ib.1, bf16[3,256,256]{2,1,0:T(8,128)(2,1)} %mass_bb.1, ...), custom_call_target="tpu_custom_call" | custom-call | flops 2818572288 | bytes 12582912 | tf_op jit(solution)/shard_map/reduce_assemble/pallas_call | solution.py:371
  37.2 0.8 %finish.1 = (f32[16,8,256]{2,1,0:T(8,128)}, f32[3,128,256]{2,1,0:T(8,128)}) custom-call(f32[16,8,256]{2,1,0:T(8,128)S(1)} %get-tuple-element.4.blocks_in, f32[3,128,256]{2,1,0:T(8,128)S(1)} %get-tuple-element.5.coupling_in), custom_call_target="tpu_custom_call" | custom-call | tf_op jit(solution)/shard_map/finish/pallas_call | solution.py:406

commit v4 on v3

--- a/solution.py
+++ b/solution.py
@@ -54,6 +54,7 @@
     ahead_in,
     home_in,
     relay_in,
+    carried,
     load_sem,
     part_sem,
     codes_in,
@@ -61,6 +62,7 @@
     row_recv,
     code_sem,
     end_sem,
+    carry_sem,
 ):
     slots, inner, width = mass_ib.shape
     own = width // n_sub
@@ -78,6 +80,15 @@
     out_sub = jnp.where(last, mirrored(sub), sub)
     in_sub = jnp.where(first, mirrored(sub), sub)
     far_grp = lax.rem(grp + X_CHIPS, n_grp)
+    carrier = lax.rem(grp, X_CHIPS) == X_CHIPS - 2
+    side_size = n_sub // 2
+    far_low = side_size - (sub // side_size) * side_size
+
+    def near_peer(turn):
+        return side_size - far_low + lax.rem(sub + turn, side_size)
+
+    def far_peer(turn):
+        return far_low + lax.rem(sub + turn, side_size)
 
     def load(j, at):
         pairs = (
@@ -126,7 +137,24 @@
         pl.semaphore_signal(barrier, inc=1, device_id={"grp": grp + (X_CHIPS - 1)}, device_id_type=MESH)
         pl.semaphore_signal(barrier, inc=1, device_id={"grp": far_grp}, device_id_type=MESH)
 
+    def greet_far(shift):
+        def one(turn, carry):
+            device = {"grp": grp + shift, "sub": far_peer(turn)}
+            pl.semaphore_signal(barrier, inc=1, device_id=device, device_id_type=MESH)
+            return carry
+
+        lax.fori_loop(0, side_size, one, 0)
+
+    @pl.when(carrier)
+    def _():
+        greet_far(1)
+
+    @pl.when(last)
+    def _():
+        greet_far(-1)
+
     greeted = n_sub + 1 + jnp.where(last, 1, 0) + jnp.where(first, 2, 0)
+    greeted += jnp.where(carrier | last, side_size, 0)
 
     used = counts[0]
 
@@ -152,15 +180,39 @@
             device_id_type=MESH,
         )
 
-    def right_copy(step):
-        peer = lax.rem(sub + step, n_sub)
+    def right_copy(peer, count, sem):
+        step = lax.rem(peer - sub + n_sub, n_sub)
         block = jnp.where(last, mirrored(peer), peer)
         return pltpu.make_async_remote_copy(
-            src_ref=placed.at[1, :, pl.ds(pl.multiple_of(block * own, own), own)],
-            dst_ref=rows_in.at[1, :, pl.ds(pl.multiple_of(step * own, own), own)],
-            send_sem=row_send.at[slots],
+            src_ref=placed.at[1, pl.ds(0, count), pl.ds(pl.multiple_of(block * own, own), own)],
+            dst_ref=rows_in.at[1, pl.ds(0, count), pl.ds(pl.multiple_of(step * own, own), own)],
+            send_sem=row_send.at[sem],
             recv_sem=row_recv.at[slots],
             device_id={"sub": peer},
+            device_id_type=MESH,
+        )
+
+    carry_low = (side_size - far_low) * own
+    carry_size = side_size * own
+
+    carry_out = pltpu.make_async_remote_copy(
+        src_ref=placed.at[1, slots - 1, pl.ds(pl.multiple_of(carry_low, own), carry_size)],
+        dst_ref=carried,
+        send_sem=carry_sem.at[0],
+        recv_sem=carry_sem.at[1],
+        device_id={"grp": grp - 1},
+        device_id_type=MESH,
+    )
+
+    def carry_on(turn):
+        peer = far_peer(turn)
+        step = lax.rem(peer - sub + n_sub, n_sub)
+        return pltpu.make_async_remote_copy(
+            src_ref=carried.at[pl.ds(pl.multiple_of(mirrored(peer) * own - carry_low, own), own)],
+            dst_ref=rows_in.at[1, slots - 1, pl.ds(pl.multiple_of(step * own, own), own)],
+            send_sem=carry_sem.at[2],
+            recv_sem=row_recv.at[slots],
+            device_id={"grp": grp + 1, "sub": peer},
             device_id_type=MESH,
         )
 
@@ -218,7 +270,10 @@
 
     lax.fori_loop(0, slots, slot, 0)
 
-    lax.fori_loop(1, n_sub, lambda step, c: (right_copy(step).start(), c)[1], 0)
+    @pl.when(last)
+    def _():
+        carry_out.start()
+
     rows_in[0, :, pl.ds(0, own)] = placed[0, :, pl.ds(pl.multiple_of(sub * own, own), own)]
     rows_in[1, :, pl.ds(0, own)] = placed[1, :, pl.ds(pl.multiple_of(out_sub * own, own), own)]
 
@@ -229,6 +284,36 @@
         return carry
 
     lax.fori_loop(0, slots, couple, 0)
+
+    @pl.when(carrier)
+    def _():
+        carry_out.wait_recv()
+        lax.fori_loop(0, side_size, lambda turn, c: (carry_on(turn).start(), c)[1], 0)
+
+    lax.fori_loop(1, side_size, lambda turn, c: (right_copy(near_peer(turn), slots, slots).start(), c)[1], 0)
+
+    @pl.when(carrier)
+    def _():
+        pltpu.make_async_remote_copy(
+            src_ref=carried,
+            dst_ref=carried,
+            send_sem=carry_sem.at[2],
+            recv_sem=carry_sem.at[1],
+            device_id={"sub": sub},
+            device_id_type=MESH,
+        ).wait_send()
+
+    def far_rows(count):
+        return lambda turn, c: (right_copy(far_peer(turn), count, slots + 1).start(), c)[1]
+
+    @pl.when(last)
+    def _():
+        lax.fori_loop(0, side_size, far_rows(slots - 1), 0)
+
+    @pl.when(jnp.logical_not(last))
+    def _():
+        lax.fori_loop(0, side_size, far_rows(slots), 0)
+
 
     others = pltpu.make_async_remote_copy(
         src_ref=code_in.at[pl.ds(1, n_sub - 1)],
@@ -245,9 +330,8 @@
     hot = jnp.concatenate([(code_all[:, j : j + 1] == target).astype(jnp.float32) for j in range(slots)] * 2, axis=0)
     hot_all[...] = hot.T.astype(jnp.bfloat16)
 
-    def arrived(side, j, sem):
-        refs = rows_in.at[side, j, pl.ds(own, width - own)]
-        copy = pltpu.make_async_remote_copy(
+    def expect(refs, sem):
+        return pltpu.make_async_remote_copy(
             src_ref=refs,
             dst_ref=refs,
             send_sem=row_send.at[sem],
@@ -255,8 +339,6 @@
             device_id={"sub": sub},
             device_id_type=MESH,
         )
-        copy.wait_recv()
-        copy.wait_send()
 
     def assemble(side):
         for r in range(0, own, 2):
@@ -287,7 +369,9 @@
         return staged.at[side, pl.ds(size, size)]
 
     for j in range(slots):
-        arrived(0, j, j)
+        left = expect(rows_in.at[0, j, pl.ds(own, width - own)], j)
+        left.wait_recv()
+        left.wait_send()
     assemble(0)
     straight = end_copy(ahead_of(0), ahead_in.at[0], 0, 0, {"grp": next_grp})
     aside = end_copy(ahead_of(0), relay_in, 1, 1, {"grp": grp - (X_CHIPS - 1)})
@@ -308,7 +392,7 @@
         aside.wait_recv()
         onward.start()
 
-    arrived(1, slice(None), slots)
+    expect(rows_in.at[1, :, pl.ds(own, width - own)], slots).wait_recv()
     assemble(1)
     ahead = end_copy(ahead_of(1), ahead_in.at[1], 2, 2, {"grp": next_grp, "sub": out_sub})
     home = end_copy(staged.at[1, pl.ds(0, size)], home_in.at[1], 3, 3, {"sub": out_sub})
@@ -340,6 +424,16 @@
 
     ahead.wait()
     write(1)
+    expect(rows_in.at[1, :, pl.ds(own, (side_size - 1) * own)], slots).wait_send()
+
+    @pl.when(last)
+    def _():
+        expect(rows_in.at[1, pl.ds(0, slots - 1), pl.ds(0, carry_size)], slots + 1).wait_send()
+        carry_out.wait_send()
+
+    @pl.when(jnp.logical_not(last))
+    def _():
+        expect(rows_in.at[1, :, pl.ds(0, carry_size)], slots + 1).wait_send()
 
 
 def finish(blocks_in, coupling_in, blocks, coupling, sems):
@@ -389,13 +483,15 @@
                 pltpu.VMEM((SIDES, NBG * own, LANES), jnp.float32),
                 pltpu.VMEM((SIDES, NBG * own, LANES), jnp.float32),
                 pltpu.VMEM((NBG * own, LANES), jnp.float32),
+                pltpu.VMEM((width // 2, LANES), jnp.float32),
                 pltpu.SemaphoreType.DMA((slots, 5)),
                 pltpu.SemaphoreType.DMA((slots, PARTS)),
                 pltpu.SMEM((slots,), jnp.int32),
-                pltpu.SemaphoreType.DMA((slots + 1,)),
+                pltpu.SemaphoreType.DMA((slots + 2,)),
                 pltpu.SemaphoreType.DMA((slots + 1,)),
                 pltpu.SemaphoreType.DMA((2,)),
                 pltpu.SemaphoreType.DMA((2, 5)),
+                pltpu.SemaphoreType.DMA((3,)),
             ],
             compiler_params=pltpu.CompilerParams(
                 collective_id=0, has_side_effects=True, vmem_limit_bytes=24 * 1024 * 1024

time: 38.2 us -> 37.7 us (0.987); the launches traced: 38.1 us -> 37.1 us
  Pallas kernels: 36.8 us -> 35.9 us
    pallas_call x1, Pallas kernels: 36 us -> 35.1 us  [per_device(): pl.pallas_call(functools.partial(body, n_grp, n_sub), out_shape=shapes, i...]
where the time goes in v4:
time: 37.7 us; the launch traced here: 37.1 us
  Pallas kernels  35.9 us (95%)
  between operations  1.29 us (3%)
    pallas_call x1, Pallas kernels, per_device(): pl.pallas_call(functools.partial(body, n_grp, n_sub), out_shape=shapes, i...  35.1 us
    pallas_call x1, Pallas kernels, per_device(): pl.pallas_call(finish, out_shape=shapes, in_specs=[near] * 2, out_specs=(...  0.8 us

profile of v4, /device:TPU:1, one launch (start us, length us, event | category | flops | bytes accessed | tf_op | source)
XLA Modules:
  0.0 37.1 jit_solution(1247874895820802739)
XLA Ops:
  1.3 35.1 %reduce_assemble.1 = (f32[16,8,256]{2,1,0:T(8,128)S(1)}, f32[3,128,256]{2,1,0:T(8,128)S(1)}) custom-call(s32[1]{0:T(128)S(6)} %copy.10.counts, s32[3]{0:T(128)} %codes_any.1, s32[3,256]{1,0:T(4,128)} %perms.1, bf16[3,1024,1024]{2,1,0:T(8,128)(2,1)} %mass_ii.1, bf16[3,1024,256]{2,1,0:T(8,128)(2,1)} %mass_ib.1, bf16[3,256,256]{2,1,0:T(8,128)(2,1)} %mass_bb.1, ...), custom_call_target="tpu_custom_call" | custom-call | flops 2818572288 | bytes 12582912 | tf_op jit(solution)/shard_map/reduce_assemble/pallas_call | solution.py:465
  36.3 0.8 %finish.1 = (f32[16,8,256]{2,1,0:T(8,128)}, f32[3,128,256]{2,1,0:T(8,128)}) custom-call(f32[16,8,256]{2,1,0:T(8,128)S(1)} %get-tuple-element.4.blocks_in, f32[3,128,256]{2,1,0:T(8,128)S(1)} %get-tuple-element.5.coupling_in), custom_call_target="tpu_custom_call" | custom-call | tf_op jit(solution)/shard_map/finish/pallas_call | solution.py:502

commit v5 on v4

--- a/solution.py
+++ b/solution.py
@@ -80,6 +80,7 @@
     out_sub = jnp.where(last, mirrored(sub), sub)
     in_sub = jnp.where(first, mirrored(sub), sub)
     far_grp = lax.rem(grp + X_CHIPS, n_grp)
+    beside = (sub // run + 1 - 2 * lax.rem(sub // run, 2)) * run + lax.rem(sub, run)
     carrier = lax.rem(grp, X_CHIPS) == X_CHIPS - 2
     side_size = n_sub // 2
     far_low = side_size - (sub // side_size) * side_size
@@ -130,12 +131,12 @@
 
     @pl.when(last)
     def _():
-        pl.semaphore_signal(barrier, inc=1, device_id={"grp": grp - (X_CHIPS - 1)}, device_id_type=MESH)
+        pl.semaphore_signal(barrier, inc=1, device_id={"grp": grp - (X_CHIPS - 1), "sub": beside}, device_id_type=MESH)
 
     @pl.when(first)
     def _():
-        pl.semaphore_signal(barrier, inc=1, device_id={"grp": grp + (X_CHIPS - 1)}, device_id_type=MESH)
-        pl.semaphore_signal(barrier, inc=1, device_id={"grp": far_grp}, device_id_type=MESH)
+        pl.semaphore_signal(barrier, inc=1, device_id={"grp": grp + (X_CHIPS - 1), "sub": beside}, device_id_type=MESH)
+        pl.semaphore_signal(barrier, inc=1, device_id={"grp": far_grp, "sub": beside}, device_id_type=MESH)
 
     def greet_far(shift):
         def one(turn, carry):
@@ -374,8 +375,8 @@
         left.wait_send()
     assemble(0)
     straight = end_copy(ahead_of(0), ahead_in.at[0], 0, 0, {"grp": next_grp})
-    aside = end_copy(ahead_of(0), relay_in, 1, 1, {"grp": grp - (X_CHIPS - 1)})
-    onward = end_copy(relay_in, ahead_in.at[0], 4, 0, {"grp": far_grp})
+    aside = end_copy(ahead_of(0), relay_in, 1, 1, {"grp": grp - (X_CHIPS - 1), "sub": beside})
+    onward = end_copy(relay_in, ahead_in.at[0], 4, 0, {"grp": far_grp, "sub": beside})
 
     @pl.when(last)
     def _():

time: 37.7 us -> 37.2 us (0.987)
  the two profiles are of different devices: /device:TPU:1 before, /device:TPU:6 now
where the time goes in v5:
time: 37.2 us; the launch traced here: 37.1 us
  Pallas kernels  35.8 us (96%)
  between operations  1.29 us (3%)
    pallas_call x1, Pallas kernels, per_device(): pl.pallas_call(functools.partial(body, n_grp, n_sub), out_shape=shapes, i...  35 us
    pallas_call x1, Pallas kernels, per_device(): pl.pallas_call(finish, out_shape=shapes, in_specs=[near] * 2, out_specs=(...  0.8 us

profile of v5, /device:TPU:6, one launch (start us, length us, event | category | flops | bytes accessed | tf_op | source)
XLA Modules:
  0.0 37.1 jit_solution(6783855815137620272)
XLA Ops:
  1.3 35.0 %reduce_assemble.1 = (f32[16,8,256]{2,1,0:T(8,128)S(1)}, f32[3,128,256]{2,1,0:T(8,128)S(1)}) custom-call(s32[1]{0:T(128)S(6)} %copy.10.counts, s32[3]{0:T(128)} %codes_any.1, s32[3,256]{1,0:T(4,128)} %perms.1, bf16[3,1024,1024]{2,1,0:T(8,128)(2,1)} %mass_ii.1, bf16[3,1024,256]{2,1,0:T(8,128)(2,1)} %mass_ib.1, bf16[3,256,256]{2,1,0:T(8,128)(2,1)} %mass_bb.1, ...), custom_call_target="tpu_custom_call" | custom-call | flops 2818572288 | bytes 12582912 | tf_op jit(solution)/shard_map/reduce_assemble/pallas_call | solution.py:466
  36.3 0.8 %finish.1 = (f32[16,8,256]{2,1,0:T(8,128)}, f32[3,128,256]{2,1,0:T(8,128)}) custom-call(f32[16,8,256]{2,1,0:T(8,128)S(1)} %get-tuple-element.4.blocks_in, f32[3,128,256]{2,1,0:T(8,128)S(1)} %get-tuple-element.5.coupling_in), custom_call_target="tpu_custom_call" | custom-call | tf_op jit(solution)/shard_map/finish/pallas_call | solution.py:503
